TPU v7x, 32 devices: a whole 2x2x4 slice. The times are simulated.
32 devices in a mesh: pix: 8 (over z, y), rep: 4 (over x, core).
Axes of the slice: x: 2, y: 2, z: 4, core: 2. Of those that a mesh axis runs over, the one named last changes fastest.
Arguments:
- interferograms: float32 [256, 131072], P(('pix', 'rep')), may hold values from -6 to 6
- epoch_pairs: int32 [2, 256], replicated, may hold values from 0 to 63, as said below
- los: float32 [3, 131072], P(None, ('pix', 'rep')), may hold values from 0.3 to 1
- patch_place: int32 [2, 4096], replicated, may hold values from 0 to 255, as said below
- patch_depth: int32 [4096], replicated, may hold values from 0 to 7
Outputs:
- predicted: float32 [64, 131072], P(None, ('pix', 'rep'))
- slip: float32 [64, 4096], P(None, ('pix', 'rep'))
Inputs may be any that keep to these rules, and one draw needn't show every extreme that they name: `epoch_pairs`: row 0 holds an interferogram's earlier epoch and row 1 its later one; the two always differ. `patch_place`: row 0 is an east cell below 256; row 1 is a north cell below 32.
All inputs are finite; a program needn't handle non-finite values.
Results may differ from a plain program's by a relative error of at most 0.0037.
Values may be sent and summed in bfloat16 or wider, within the bound.
A program may use at most 64 MiB of HBM per device.

v0:
```python
import jax
import jax.numpy as jnp
from jax import lax
from jax.sharding import PartitionSpec as P

NEP = 64
IMG_W = 1024
pixel_step = 0.1
patch_step = 0.4
damping = 0.5
depth_base = 0.5
depth_step = 0.25


def sbas_inverse(epoch_pairs, epochs_count):
    epochs = lax.iota(jnp.int32, epochs_count)
    design = (epochs[None, :] == epoch_pairs[1][:, None]).astype(jnp.float32) - (
        epochs[None, :] == epoch_pairs[0][:, None]
    ).astype(jnp.float32)
    normal = jnp.dot(design.T, design, precision=lax.Precision.HIGHEST) + damping * jnp.eye(
        epochs_count, dtype=jnp.float32
    )
    factor = jnp.linalg.cholesky(normal)
    return jax.scipy.linalg.cho_solve((factor, True), design.T)


def green_tile(pixel, los_rows, patch_place, patch_depth):
    column = (pixel % IMG_W).astype(jnp.float32)
    line = (pixel // IMG_W).astype(jnp.float32)
    xpos = (column + 0.5) * pixel_step
    ypos = (line + 0.5) * pixel_step
    patch_x = (patch_place[0].astype(jnp.float32) + 0.5) * patch_step
    patch_y = (patch_place[1].astype(jnp.float32) + 0.5) * patch_step
    patch_z = depth_base + depth_step * patch_depth.astype(jnp.float32)
    delta_x = xpos[:, None] - patch_x[None, :]
    delta_y = ypos[:, None] - patch_y[None, :]
    delta_z = patch_z[None, :]
    dist_sq = delta_x * delta_x + delta_y * delta_y + delta_z * delta_z
    toward = (
        los_rows[0][:, None] * delta_x
        + los_rows[1][:, None] * delta_y
        + los_rows[2][:, None] * delta_z
    )
    return (delta_z * toward / (dist_sq * jnp.sqrt(dist_sq))).astype(jnp.bfloat16)


def on_device(interferograms, epoch_pairs, los, patch_place, patch_depth):
    devices = lax.axis_size(("pix", "rep"))
    ifg_dev, total = interferograms.shape
    pix_dev = total // devices
    epochs_count = NEP
    npatch = patch_depth.shape[0]
    own = npatch // devices
    pseudo = sbas_inverse(epoch_pairs, epochs_count)
    pieces = interferograms.reshape(ifg_dev, devices, pix_dev)
    series = jnp.dot(
        pseudo,
        lax.all_to_all(pieces, ("pix", "rep"), split_axis=1, concat_axis=0, tiled=True)[:, 0, :],
        precision=lax.Precision.HIGHEST,
        preferred_element_type=jnp.float32,
    )
    anchor = lax.axis_index(("pix", "rep")) * pix_dev
    width = min(512, pix_dev)
    count = pix_dev // width

    def tile_at(index):
        start = index * width
        pixel = anchor + start + lax.iota(jnp.int32, width)
        los_rows = lax.dynamic_slice_in_dim(los, start, width, 1)
        return (green_tile(pixel, los_rows, patch_place, patch_depth), start)

    def first_step(index, carry):
        rhs, bound = carry
        tile, start = tile_at(index)
        resid = lax.dynamic_slice_in_dim(series, start, width, 1).astype(jnp.bfloat16)
        rhs = rhs + jnp.dot(resid, tile, preferred_element_type=jnp.float32)
        magnitude = jnp.abs(tile)
        weight = jnp.sum(magnitude.astype(jnp.float32), axis=1).astype(jnp.bfloat16)
        bound = bound + jnp.dot(weight[None, :], magnitude, preferred_element_type=jnp.float32)
        return (rhs, bound)

    zero_rhs = jnp.zeros((epochs_count, npatch), jnp.float32)
    zero_bound = jnp.zeros((1, npatch), jnp.float32)
    rhs, bound = lax.fori_loop(0, count, first_step, (zero_rhs, zero_bound))
    rhs_all, bound_all = lax.psum((rhs, bound), ("pix", "rep"))
    slip_all = rhs_all / bound_all
    sweep_slip_half = slip_all.astype(jnp.bfloat16)

    def sweep_step(index, rhs_now):
        tile, start = tile_at(index)
        guess = lax.dot_general(
            sweep_slip_half, tile, (((1,), (1,)), ((), ())), preferred_element_type=jnp.float32
        )
        resid = (lax.dynamic_slice_in_dim(series, start, width, 1) - guess).astype(jnp.bfloat16)
        return rhs_now + jnp.dot(resid, tile, preferred_element_type=jnp.float32)

    rhs = lax.fori_loop(0, count, sweep_step, zero_rhs)
    slip_all = slip_all + lax.psum(rhs, ("pix", "rep")) / bound_all
    slip_half = slip_all.astype(jnp.bfloat16)
    slip_own = lax.dynamic_slice_in_dim(slip_all, lax.axis_index(("pix", "rep")) * own, own, 1)

    def final_step(index, predicted):
        tile, start = tile_at(index)
        block = lax.dot_general(
            slip_half, tile, (((1,), (1,)), ((), ())), preferred_element_type=jnp.float32
        )
        return lax.dynamic_update_slice_in_dim(predicted, block, start, 1)

    predicted = lax.fori_loop(0, count, final_step, jnp.zeros((epochs_count, pix_dev), jnp.float32))
    return (predicted, slip_own)


def solution(mesh):
    placed = (P(("pix", "rep"), None), P(), P(None, ("pix", "rep")), P(), P())
    return jax.shard_map(
        on_device,
        mesh=mesh,
        in_specs=placed,
        out_specs=(P(None, ("pix", "rep")), P(None, ("pix", "rep"))),
        check_vma=False,
    )
```

profile of v0, /device:TPU:0, one launch (start us, length us, event | category | flops | bytes accessed | tf_op | source)
XLA Modules:
  0.0 731.8 jit_solution(1607313868562399574)
XLA Ops:
  7.2 7.5 %all-to-all-start = ((f32[8,32,4096]{2,0,1:T(8,128)}), f32[8,32,4096]{2,0,1:T(8,128)}, u32[]{:S(2)}, u32[]{:S(2)}) async-start(f32[8,32,4096]{2,0,1:T(8,128)} %bitcast.110), calls=%async_computation | async-start | bytes 8388608 | tf_op jit(solution)/shard_map/all_to_all | solution.py:58
  28.2 80.2 %all-to-all-done = f32[8,32,4096]{2,0,1:T(8,128)} async-done(((f32[8,32,4096]{2,0,1:T(8,128)}), f32[8,32,4096]{2,0,1:T(8,128)}, u32[]{:S(2)}, u32[]{:S(2)}) %all-to-all-start) | async-done | bytes 4194336 | tf_op jit(solution)/shard_map/all_to_all | solution.py:58
  114.1 168.4 %while.53 = (s32[]{:T(128)}, f32[64,4096]{1,0:T(8,128)S(1)}, f32[1,4096]{1,0:T(1,128)S(1)}, bf16[64,4096]{1,0:T(8,128)(2,1)S(1)}, f32[1,4096]{1,0:T(1,128)S(1)},...) while((s32[]{:T(128)}, f32[64,4096]{1,0:T(8,128)S(1)}, ...), condition=%wide.region_4.5_spmd.clone, body=%wide.region_2.4_spmd.clone.sunk | while | flops 373867008 | bytes 2590974 | solution.py:84
  115.3 6.6 convolution_add_fusion.6
  121.9 6.8 abs_reduce_fusion.2
  136.3 6.6 convolution_add_fusion.6
  142.8 6.8 abs_reduce_fusion.2
  157.3 6.6 convolution_add_fusion.6
  163.8 6.8 abs_reduce_fusion.2
  178.2 6.6 convolution_add_fusion.6
  184.8 6.8 abs_reduce_fusion.2
  199.2 6.6 convolution_add_fusion.6
  205.8 6.8 abs_reduce_fusion.2
  220.2 6.6 convolution_add_fusion.6
  226.8 6.8 abs_reduce_fusion.2
  241.2 6.6 convolution_add_fusion.6
  247.7 6.8 abs_reduce_fusion.2
  262.1 6.6 convolution_add_fusion.6
  268.7 6.8 abs_reduce_fusion.2
  283.6 38.4 %psum.22 = f32[4096]{0:T(1024)S(1)} all-reduce(f32[4096]{0:T(1024)S(1)} %bitcast.147), channel_id=1, replica_groups=mesh['pix'=8,'rep'=4] {'pix','rep'}, use_global_device_ids=true, to_apply=%region_6.7 | all-reduce | flops 4096 | bytes 32768 | tf_op jit(solution)/shard_map/psum | solution.py:85
  322.0 92.1 %all-reduce.3.cloned.1.call-done = f32[64,4096]{1,0:T(8,128)} async-done(((f32[64,4096]{1,0:T(8,128)}), f32[64,4096]{1,0:T(8,128)}) %all-reduce.3.cloned.1.call-update) | async-done | bytes 1048592 | tf_op jit(solution)/shard_map/psum | solution.py:85
  415.4 117.2 %while.54 = (s32[]{:T(128)}, f32[64,4096]{1,0:T(8,128)S(1)}, f32[64,4096]{1,0:T(8,128)}, f32[1,4096]{1,0:T(1,128)S(1)}, f32[3,4096]{1,0:T(4,128)}, /*index=5*/s3...) while((s32[]{:T(128)}, f32[64,4096]{1,0:T(8,128)S(1)}, ...), condition=%wide.region_8.9_spmd.clone, body=%wide.region_7.8_spmd.clone.sunk | while | flops 600417280 | bytes 3068157 | solution.py:97
  416.4 13.6 %convolution_add_fusion.8 = f32[64,4096]{1,0:T(8,128)S(1)} fusion(f32[4096]{0:T(1024)S(1)} %mul.1511, f32[512]{0:T(512)S(1)} %bitcast.143, f32[4096]{0:T(1024)S(1)} %bitcast.128, f32[512]{0:T(512)S(1)} %get-tuple-element.1055, f32[512]{0:T(512)S(1)} %bitcast.142, f32[4096]{0:T(1024)S(1)} %bitcast.129, f32[512]{0:T(512)S(1)} %get-tuple-element.1058, ...), kind=kOutput, calls=%fused_computation.86.clone.1 | convolution fusion | flops 600375296 | bytes 2904069 | tf_op jit(solution)/shard_map/while/body/eval_jaxpr/dot_general | solution.py:95
  431.0 13.6 %convolution_add_fusion.8 = f32[64,4096]{1,0:T(8,128)S(1)} fusion(f32[4096]{0:T(1024)S(1)} %mul.1511, f32[512]{0:T(512)S(1)} %bitcast.143, f32[4096]{0:T(1024)S(1)} %bitcast.128, f32[512]{0:T(512)S(1)} %get-tuple-element.1055, f32[512]{0:T(512)S(1)} %bitcast.142, f32[4096]{0:T(1024)S(1)} %bitcast.129, f32[512]{0:T(512)S(1)} %get-tuple-element.1058, ...), kind=kOutput, calls=%fused_computation.86.clone.1 | convolution fusion | flops 600375296 | bytes 2904069 | tf_op jit(solution)/shard_map/while/body/eval_jaxpr/dot_general | solution.py:95
  445.6 13.6 %convolution_add_fusion.8 = f32[64,4096]{1,0:T(8,128)S(1)} fusion(f32[4096]{0:T(1024)S(1)} %mul.1511, f32[512]{0:T(512)S(1)} %bitcast.143, f32[4096]{0:T(1024)S(1)} %bitcast.128, f32[512]{0:T(512)S(1)} %get-tuple-element.1055, f32[512]{0:T(512)S(1)} %bitcast.142, f32[4096]{0:T(1024)S(1)} %bitcast.129, f32[512]{0:T(512)S(1)} %get-tuple-element.1058, ...), kind=kOutput, calls=%fused_computation.86.clone.1 | convolution fusion | flops 600375296 | bytes 2904069 | tf_op jit(solution)/shard_map/while/body/eval_jaxpr/dot_general | solution.py:95
  460.3 13.6 %convolution_add_fusion.8 = f32[64,4096]{1,0:T(8,128)S(1)} fusion(f32[4096]{0:T(1024)S(1)} %mul.1511, f32[512]{0:T(512)S(1)} %bitcast.143, f32[4096]{0:T(1024)S(1)} %bitcast.128, f32[512]{0:T(512)S(1)} %get-tuple-element.1055, f32[512]{0:T(512)S(1)} %bitcast.142, f32[4096]{0:T(1024)S(1)} %bitcast.129, f32[512]{0:T(512)S(1)} %get-tuple-element.1058, ...), kind=kOutput, calls=%fused_computation.86.clone.1 | convolution fusion | flops 600375296 | bytes 2904069 | tf_op jit(solution)/shard_map/while/body/eval_jaxpr/dot_general | solution.py:95
  474.9 13.6 %convolution_add_fusion.8 = f32[64,4096]{1,0:T(8,128)S(1)} fusion(f32[4096]{0:T(1024)S(1)} %mul.1511, f32[512]{0:T(512)S(1)} %bitcast.143, f32[4096]{0:T(1024)S(1)} %bitcast.128, f32[512]{0:T(512)S(1)} %get-tuple-element.1055, f32[512]{0:T(512)S(1)} %bitcast.142, f32[4096]{0:T(1024)S(1)} %bitcast.129, f32[512]{0:T(512)S(1)} %get-tuple-element.1058, ...), kind=kOutput, calls=%fused_computation.86.clone.1 | convolution fusion | flops 600375296 | bytes 2904069 | tf_op jit(solution)/shard_map/while/body/eval_jaxpr/dot_general | solution.py:95
  489.5 13.6 %convolution_add_fusion.8 = f32[64,4096]{1,0:T(8,128)S(1)} fusion(f32[4096]{0:T(1024)S(1)} %mul.1511, f32[512]{0:T(512)S(1)} %bitcast.143, f32[4096]{0:T(1024)S(1)} %bitcast.128, f32[512]{0:T(512)S(1)} %get-tuple-element.1055, f32[512]{0:T(512)S(1)} %bitcast.142, f32[4096]{0:T(1024)S(1)} %bitcast.129, f32[512]{0:T(512)S(1)} %get-tuple-element.1058, ...), kind=kOutput, calls=%fused_computation.86.clone.1 | convolution fusion | flops 600375296 | bytes 2904069 | tf_op jit(solution)/shard_map/while/body/eval_jaxpr/dot_general | solution.py:95
  504.1 13.6 %convolution_add_fusion.8 = f32[64,4096]{1,0:T(8,128)S(1)} fusion(f32[4096]{0:T(1024)S(1)} %mul.1511, f32[512]{0:T(512)S(1)} %bitcast.143, f32[4096]{0:T(1024)S(1)} %bitcast.128, f32[512]{0:T(512)S(1)} %get-tuple-element.1055, f32[512]{0:T(512)S(1)} %bitcast.142, f32[4096]{0:T(1024)S(1)} %bitcast.129, f32[512]{0:T(512)S(1)} %get-tuple-element.1058, ...), kind=kOutput, calls=%fused_computation.86.clone.1 | convolution fusion | flops 600375296 | bytes 2904069 | tf_op jit(solution)/shard_map/while/body/eval_jaxpr/dot_general | solution.py:95
  518.8 13.6 %convolution_add_fusion.8 = f32[64,4096]{1,0:T(8,128)S(1)} fusion(f32[4096]{0:T(1024)S(1)} %mul.1511, f32[512]{0:T(512)S(1)} %bitcast.143, f32[4096]{0:T(1024)S(1)} %bitcast.128, f32[512]{0:T(512)S(1)} %get-tuple-element.1055, f32[512]{0:T(512)S(1)} %bitcast.142, f32[4096]{0:T(1024)S(1)} %bitcast.129, f32[512]{0:T(512)S(1)} %get-tuple-element.1058, ...), kind=kOutput, calls=%fused_computation.86.clone.1 | convolution fusion | flops 600375296 | bytes 2904069 | tf_op jit(solution)/shard_map/while/body/eval_jaxpr/dot_general | solution.py:95
  533.5 129.8 %all-reduce.5.cloned.1.call-done = f32[64,4096]{1,0:T(8,128)} async-done(((f32[64,4096]{1,0:T(8,128)}), f32[64,4096]{1,0:T(8,128)}) %all-reduce.5.cloned.1.call-update) | async-done | bytes 1048592 | tf_op jit(solution)/shard_map/psum | solution.py:98
  664.8 59.0 %while.52 = (s32[]{:T(128)}, f32[64,4096]{1,0:T(8,128)S(1)}, f32[1,4096]{1,0:T(1,128)S(1)}, f32[3,4096]{1,0:T(4,128)}, s32[]{:T(128)}, /*index=5*/f32[1,4096]{1,...) while((s32[]{:T(128)}, f32[64,4096]{1,0:T(8,128)S(1)}, ...), condition=%wide.region_11.12_spmd, body=%wide.region_10.11_spmd.sunk | while | flops 299934720 | bytes 895211 | solution.py:109
  (185 shorter events, 151.6 us)
Async XLA Ops:
  7.2 7.6 %copy-start.7 = (s32[2,256]{1,0:T(2,128)S(1)}, s32[2,256]{1,0:T(2,128)}, u32[]{:S(2)}) copy-start(s32[2,256]{1,0:T(2,128)} %param.12) | copy-start | bytes 6148
  7.2 20.3 %copy-start.6 = (s32[4096]{0:T(1024)S(1)}, s32[4096]{0:T(1024)}, u32[]{:S(2)}) copy-start(s32[4096]{0:T(1024)} %param.15) | copy-start | bytes 49156
  7.2 20.9 %copy-start.5 = (s32[2,4096]{1,0:T(2,128)S(1)}, s32[2,4096]{1,0:T(2,128)}, u32[]{:S(2)}) copy-start(s32[2,4096]{1,0:T(2,128)} %param.14) | copy-start | bytes 98308
  7.2 101.2 %all-to-all-start = ((f32[8,32,4096]{2,0,1:T(8,128)}), f32[8,32,4096]{2,0,1:T(8,128)}, u32[]{:S(2)}, u32[]{:S(2)}) async-start(f32[8,32,4096]{2,0,1:T(8,128)} %bitcast.110), calls=%async_computation | async-start | bytes 8388608 | tf_op jit(solution)/shard_map/all_to_all | solution.py:58
  14.7 399.4 %all-reduce.3.cloned.1.call-start = ((), (), s32[]{:S(2)}) async-start(), calls=%async_computation.1 | async-start | bytes 2097152 | tf_op jit(solution)/shard_map/psum | solution.py:85
  282.5 1.0 copy-start.1
  283.5 379.8 %all-reduce.5.cloned.1.call-start = ((), (), s32[]{:S(2)}) async-start(), calls=%async_computation.2 | async-start | bytes 2097152 | tf_op jit(solution)/shard_map/psum | solution.py:98
  322.0 93.4 %copy-start.4 = (f32[4096]{0:T(1024)}, f32[4096]{0:T(1024)S(1)}, u32[]{:S(2)}) copy-start(f32[4096]{0:T(1024)S(1)} %psum.22) | copy-start | bytes 49156
  415.4 248.0 %copy-start = (f32[64,4096]{1,0:T(8,128)S(1)}, f32[64,4096]{1,0:T(8,128)}, u32[]{:S(2)}) copy-start(f32[64,4096]{1,0:T(8,128)} %all-reduce.3.cloned.1.call-done) | copy-start | bytes 3145732
  532.5 1.0 copy-start.2
  723.8 1.0 copy-start.3
Sparse Core Ops, SparseCore 0:
  283.7 130.3 all-reduce.2
  533.7 129.6 all-reduce.4
where the time goes:
time: 738 us; the launch traced here: 732 us
  waiting for transfers between devices  302 us (41%)
  matrix products  271 us (37%)
  other arithmetic  71.6 us (10%)
  blocking collectives  38.4 us (5%)
  local copies, waits for them, and re-layouts  24.6 us (3%)
  between operations  14.5 us (2%)
  starting transfers between devices  7.54 us (1%)
    psum x1, waiting for transfers between devices, on_device(): slip_all = slip_all + lax.psum(rhs, ('pix', 'rep')) / bound_all  130 us
    dot_general x8, matrix products, sweep_step(): return rhs_now + jnp.dot(resid, tile, preferred_element_type=jnp.float32)  109 us
    psum x1, waiting for transfers between devices, on_device(): rhs_all, bound_all = lax.psum((rhs, bound), ('pix', 'rep'))  92.1 us
    all_to_all x1, waiting for transfers between devices, on_device(): lax.all_to_all(pieces, ('pix', 'rep'), split_axis=1, concat_axis=0, tiled...  80.2 us
    reduce_sum x8, other arithmetic, first_step(): weight = jnp.sum(magnitude.astype(jnp.float32), axis=1).astype(jnp.bfloat16)  54.8 us
    dot_general x8, matrix products, first_step(): rhs = rhs + jnp.dot(resid, tile, preferred_element_type=jnp.float32)  52.5 us
    dot_general x8, matrix products, first_step(): jnp.dot(weight[None, :], magnitude, preferred_element_type=jnp.float32)  52.4 us
    dot_general x8, matrix products, final_step(): lax.dot_general(slip_half, tile, (((1,), (1,)), ((), ())), preferred_elem...  50.8 us
  transfers between devices with their start and end apart: 3, of which 3 were waited for; matrix products, arithmetic and copies ran while one was open for 2% of the time, Pallas kernels for 0%

commit v1 on v0

--- a/solution.py
+++ b/solution.py
@@ -55,7 +55,15 @@
     pieces = interferograms.reshape(ifg_dev, devices, pix_dev)
     series = jnp.dot(
         pseudo,
-        lax.all_to_all(pieces, ("pix", "rep"), split_axis=1, concat_axis=0, tiled=True)[:, 0, :],
+        jnp.concatenate(
+            lax.all_to_all(
+                jnp.stack(jnp.split(pieces, lax.axis_size(("pix", "rep")), axis=1)),
+                ("pix", "rep"),
+                0,
+                0,
+            ),
+            axis=0,
+        )[:, 0, :],
         precision=lax.Precision.HIGHEST,
         preferred_element_type=jnp.float32,
     )

time: 738 us -> 774 us (1.049)
  local copies, waits for them, and re-layouts: 24.6 us -> 60.5 us
    unnamed x16 -> x51, local copies, waits for them, and re-layouts: 2.28 us -> 37.5 us
where the time goes in v1:
time: 774 us; the launch traced here: 768 us
  waiting for transfers between devices  302 us (39%)
  matrix products  271 us (35%)
  other arithmetic  71.6 us (9%)
  local copies, waits for them, and re-layouts  60.5 us (8%)
  blocking collectives  38.4 us (5%)
  between operations  14.5 us (2%)
    psum x1, waiting for transfers between devices, on_device(): slip_all = slip_all + lax.psum(rhs, ('pix', 'rep')) / bound_all  130 us
    dot_general x8, matrix products, sweep_step(): return rhs_now + jnp.dot(resid, tile, preferred_element_type=jnp.float32)  109 us
    psum x1, waiting for transfers between devices, on_device(): rhs_all, bound_all = lax.psum((rhs, bound), ('pix', 'rep'))  92 us
    all_to_all x1, waiting for transfers between devices, on_device(): lax.all_to_all(jnp.stack(jnp.split(pieces, lax.axis_size(('pix', 'rep')),...  80.2 us
    reduce_sum x8, other arithmetic, first_step(): weight = jnp.sum(magnitude.astype(jnp.float32), axis=1).astype(jnp.bfloat16)  54.8 us
    dot_general x8, matrix products, first_step(): rhs = rhs + jnp.dot(resid, tile, preferred_element_type=jnp.float32)  52.5 us
    dot_general x8, matrix products, first_step(): jnp.dot(weight[None, :], magnitude, preferred_element_type=jnp.float32)  52.4 us
    dot_general x8, matrix products, final_step(): lax.dot_general(slip_half, tile, (((1,), (1,)), ((), ())), preferred_elem...  50.8 us
  transfers between devices with their start and end apart: 3, of which 3 were waited for; matrix products, arithmetic and copies ran while one was open for 2% of the time, Pallas kernels for 0%

profile of v1, /device:TPU:0, one launch (start us, length us, event | category | flops | bytes accessed | tf_op | source)
XLA Modules:
  0.0 767.8 jit_solution(6884635113125099276)
XLA Ops:
  43.1 7.5 all-to-all-start
  64.1 80.2 %all-to-all-done = f32[32,8,1,4096]{3,1,2,0:T(8,128)} async-done(((f32[32,8,1,4096]{3,1,2,0:T(8,128)}), f32[32,8,1,4096]{3,1,2,0:T(8,128)}, u32[]{:S(2)}, u32[]{:S(2)}) %all-to-all-start) | async-done | bytes 4194336 | tf_op jit(solution)/shard_map/all_to_all | solution.py:59
  150.1 168.4 %while.53 = (s32[]{:T(128)}, f32[64,4096]{1,0:T(8,128)S(1)}, f32[1,4096]{1,0:T(1,128)S(1)}, bf16[64,4096]{1,0:T(8,128)(2,1)S(1)}, f32[1,4096]{1,0:T(1,128)S(1)},...) while((s32[]{:T(128)}, f32[64,4096]{1,0:T(8,128)S(1)}, ...), condition=%wide.region_4.5_spmd.clone, body=%wide.region_2.4_spmd.clone.sunk | while | flops 373867008 | bytes 2590974 | solution.py:92
  151.2 6.6 convolution_add_fusion.6
  157.8 6.8 abs_reduce_fusion.2
  172.2 6.6 convolution_add_fusion.6
  178.8 6.8 abs_reduce_fusion.2
  193.2 6.6 convolution_add_fusion.6
  199.8 6.8 abs_reduce_fusion.2
  214.2 6.6 convolution_add_fusion.6
  220.7 6.8 abs_reduce_fusion.2
  235.2 6.6 convolution_add_fusion.6
  241.7 6.8 abs_reduce_fusion.2
  256.1 6.6 convolution_add_fusion.6
  262.7 6.8 abs_reduce_fusion.2
  277.1 6.6 convolution_add_fusion.6
  283.7 6.8 abs_reduce_fusion.2
  298.1 6.6 convolution_add_fusion.6
  304.6 6.8 abs_reduce_fusion.2
  319.5 38.4 %psum.22 = f32[4096]{0:T(1024)S(1)} all-reduce(f32[4096]{0:T(1024)S(1)} %bitcast.302), channel_id=1, replica_groups=mesh['pix'=8,'rep'=4] {'pix','rep'}, use_global_device_ids=true, to_apply=%region_6.7 | all-reduce | flops 4096 | bytes 32768 | tf_op jit(solution)/shard_map/psum | solution.py:93
  357.9 92.0 %all-reduce.3.cloned.1.call-done = f32[64,4096]{1,0:T(8,128)} async-done(((f32[64,4096]{1,0:T(8,128)}), f32[64,4096]{1,0:T(8,128)}) %all-reduce.3.cloned.1.call-update) | async-done | bytes 1048592 | tf_op jit(solution)/shard_map/psum | solution.py:93
  451.3 117.2 %while.54 = (s32[]{:T(128)}, f32[64,4096]{1,0:T(8,128)S(1)}, f32[64,4096]{1,0:T(8,128)}, f32[1,4096]{1,0:T(1,128)S(1)}, f32[3,4096]{1,0:T(4,128)}, /*index=5*/s3...) while((s32[]{:T(128)}, f32[64,4096]{1,0:T(8,128)S(1)}, ...), condition=%wide.region_8.9_spmd.clone, body=%wide.region_7.8_spmd.clone.sunk | while | flops 600417280 | bytes 3068157 | solution.py:105
  452.3 13.6 %convolution_add_fusion.8 = f32[64,4096]{1,0:T(8,128)S(1)} fusion(f32[4096]{0:T(1024)S(1)} %mul.1511, f32[512]{0:T(512)S(1)} %bitcast.298, f32[4096]{0:T(1024)S(1)} %bitcast.283, f32[512]{0:T(512)S(1)} %get-tuple-element.1055, f32[512]{0:T(512)S(1)} %bitcast.297, f32[4096]{0:T(1024)S(1)} %bitcast.284, f32[512]{0:T(512)S(1)} %get-tuple-element.1058, ...), kind=kOutput, calls=%fused_computation.86.clone.1 | convolution fusion | flops 600375296 | bytes 2904069 | tf_op jit(solution)/shard_map/while/body/eval_jaxpr/dot_general | solution.py:103
  466.9 13.6 %convolution_add_fusion.8 = f32[64,4096]{1,0:T(8,128)S(1)} fusion(f32[4096]{0:T(1024)S(1)} %mul.1511, f32[512]{0:T(512)S(1)} %bitcast.298, f32[4096]{0:T(1024)S(1)} %bitcast.283, f32[512]{0:T(512)S(1)} %get-tuple-element.1055, f32[512]{0:T(512)S(1)} %bitcast.297, f32[4096]{0:T(1024)S(1)} %bitcast.284, f32[512]{0:T(512)S(1)} %get-tuple-element.1058, ...), kind=kOutput, calls=%fused_computation.86.clone.1 | convolution fusion | flops 600375296 | bytes 2904069 | tf_op jit(solution)/shard_map/while/body/eval_jaxpr/dot_general | solution.py:103
  481.5 13.6 %convolution_add_fusion.8 = f32[64,4096]{1,0:T(8,128)S(1)} fusion(f32[4096]{0:T(1024)S(1)} %mul.1511, f32[512]{0:T(512)S(1)} %bitcast.298, f32[4096]{0:T(1024)S(1)} %bitcast.283, f32[512]{0:T(512)S(1)} %get-tuple-element.1055, f32[512]{0:T(512)S(1)} %bitcast.297, f32[4096]{0:T(1024)S(1)} %bitcast.284, f32[512]{0:T(512)S(1)} %get-tuple-element.1058, ...), kind=kOutput, calls=%fused_computation.86.clone.1 | convolution fusion | flops 600375296 | bytes 2904069 | tf_op jit(solution)/shard_map/while/body/eval_jaxpr/dot_general | solution.py:103
  496.2 13.6 %convolution_add_fusion.8 = f32[64,4096]{1,0:T(8,128)S(1)} fusion(f32[4096]{0:T(1024)S(1)} %mul.1511, f32[512]{0:T(512)S(1)} %bitcast.298, f32[4096]{0:T(1024)S(1)} %bitcast.283, f32[512]{0:T(512)S(1)} %get-tuple-element.1055, f32[512]{0:T(512)S(1)} %bitcast.297, f32[4096]{0:T(1024)S(1)} %bitcast.284, f32[512]{0:T(512)S(1)} %get-tuple-element.1058, ...), kind=kOutput, calls=%fused_computation.86.clone.1 | convolution fusion | flops 600375296 | bytes 2904069 | tf_op jit(solution)/shard_map/while/body/eval_jaxpr/dot_general | solution.py:103
  510.8 13.6 %convolution_add_fusion.8 = f32[64,4096]{1,0:T(8,128)S(1)} fusion(f32[4096]{0:T(1024)S(1)} %mul.1511, f32[512]{0:T(512)S(1)} %bitcast.298, f32[4096]{0:T(1024)S(1)} %bitcast.283, f32[512]{0:T(512)S(1)} %get-tuple-element.1055, f32[512]{0:T(512)S(1)} %bitcast.297, f32[4096]{0:T(1024)S(1)} %bitcast.284, f32[512]{0:T(512)S(1)} %get-tuple-element.1058, ...), kind=kOutput, calls=%fused_computation.86.clone.1 | convolution fusion | flops 600375296 | bytes 2904069 | tf_op jit(solution)/shard_map/while/body/eval_jaxpr/dot_general | solution.py:103
  525.4 13.6 %convolution_add_fusion.8 = f32[64,4096]{1,0:T(8,128)S(1)} fusion(f32[4096]{0:T(1024)S(1)} %mul.1511, f32[512]{0:T(512)S(1)} %bitcast.298, f32[4096]{0:T(1024)S(1)} %bitcast.283, f32[512]{0:T(512)S(1)} %get-tuple-element.1055, f32[512]{0:T(512)S(1)} %bitcast.297, f32[4096]{0:T(1024)S(1)} %bitcast.284, f32[512]{0:T(512)S(1)} %get-tuple-element.1058, ...), kind=kOutput, calls=%fused_computation.86.clone.1 | convolution fusion | flops 600375296 | bytes 2904069 | tf_op jit(solution)/shard_map/while/body/eval_jaxpr/dot_general | solution.py:103
  540.0 13.6 %convolution_add_fusion.8 = f32[64,4096]{1,0:T(8,128)S(1)} fusion(f32[4096]{0:T(1024)S(1)} %mul.1511, f32[512]{0:T(512)S(1)} %bitcast.298, f32[4096]{0:T(1024)S(1)} %bitcast.283, f32[512]{0:T(512)S(1)} %get-tuple-element.1055, f32[512]{0:T(512)S(1)} %bitcast.297, f32[4096]{0:T(1024)S(1)} %bitcast.284, f32[512]{0:T(512)S(1)} %get-tuple-element.1058, ...), kind=kOutput, calls=%fused_computation.86.clone.1 | convolution fusion | flops 600375296 | bytes 2904069 | tf_op jit(solution)/shard_map/while/body/eval_jaxpr/dot_general | solution.py:103
  554.7 13.6 %convolution_add_fusion.8 = f32[64,4096]{1,0:T(8,128)S(1)} fusion(f32[4096]{0:T(1024)S(1)} %mul.1511, f32[512]{0:T(512)S(1)} %bitcast.298, f32[4096]{0:T(1024)S(1)} %bitcast.283, f32[512]{0:T(512)S(1)} %get-tuple-element.1055, f32[512]{0:T(512)S(1)} %bitcast.297, f32[4096]{0:T(1024)S(1)} %bitcast.284, f32[512]{0:T(512)S(1)} %get-tuple-element.1058, ...), kind=kOutput, calls=%fused_computation.86.clone.1 | convolution fusion | flops 600375296 | bytes 2904069 | tf_op jit(solution)/shard_map/while/body/eval_jaxpr/dot_general | solution.py:103
  569.4 129.8 %all-reduce.5.cloned.1.call-done = f32[64,4096]{1,0:T(8,128)} async-done(((f32[64,4096]{1,0:T(8,128)}), f32[64,4096]{1,0:T(8,128)}) %all-reduce.5.cloned.1.call-update) | async-done | bytes 1048592 | tf_op jit(solution)/shard_map/psum | solution.py:106
  700.7 59.0 %while.52 = (s32[]{:T(128)}, f32[64,4096]{1,0:T(8,128)S(1)}, f32[1,4096]{1,0:T(1,128)S(1)}, f32[3,4096]{1,0:T(4,128)}, s32[]{:T(128)}, /*index=5*/f32[1,4096]{1,...) while((s32[]{:T(128)}, f32[64,4096]{1,0:T(8,128)S(1)}, ...), condition=%wide.region_11.12_spmd, body=%wide.region_10.11_spmd.sunk | while | flops 299934720 | bytes 895211 | solution.py:117
  (221 shorter events, 187.6 us)
Async XLA Ops:
  7.2 25.3 %copy-start = (f32[8,131072]{1,0:T(8,128)S(1)}, f32[8,131072]{1,0:T(8,128)}, u32[]{:S(2)}) copy-start(f32[8,131072]{1,0:T(8,128)} %param.11) | copy-start | bytes 12582916
  43.1 7.5 copy-start.9
  43.1 20.3 %copy-start.8 = (s32[4096]{0:T(1024)S(1)}, s32[4096]{0:T(1024)}, u32[]{:S(2)}) copy-start(s32[4096]{0:T(1024)} %param.15) | copy-start | bytes 49156
  43.1 20.9 %copy-start.7 = (s32[2,4096]{1,0:T(2,128)S(1)}, s32[2,4096]{1,0:T(2,128)}, u32[]{:S(2)}) copy-start(s32[2,4096]{1,0:T(2,128)} %param.14) | copy-start | bytes 98308
  43.1 101.2 %all-to-all-start = ((f32[32,8,1,4096]{3,1,2,0:T(8,128)}), f32[32,8,1,4096]{3,1,2,0:T(8,128)}, u32[]{:S(2)}, u32[]{:S(2)}) async-start(f32[32,8,1,4096]{3,1,2,0:T(8,128)} %fusion.79), calls=%async_computation | async-start | bytes 8388608 | tf_op jit(solution)/shard_map/all_to_all | solution.py:59
  50.6 399.3 %all-reduce.3.cloned.1.call-start = ((), (), s32[]{:S(2)}) async-start(), calls=%async_computation.1 | async-start | bytes 2097152 | tf_op jit(solution)/shard_map/psum | solution.py:93
  318.4 1.0 copy-start.2
  319.5 379.8 %all-reduce.5.cloned.1.call-start = ((), (), s32[]{:S(2)}) async-start(), calls=%async_computation.2 | async-start | bytes 2097152 | tf_op jit(solution)/shard_map/psum | solution.py:106
  357.9 93.3 %copy-start.5 = (f32[4096]{0:T(1024)}, f32[4096]{0:T(1024)S(1)}, u32[]{:S(2)}) copy-start(f32[4096]{0:T(1024)S(1)} %psum.22) | copy-start | bytes 49156
  451.2 248.0 %copy-start.1 = (f32[64,4096]{1,0:T(8,128)S(1)}, f32[64,4096]{1,0:T(8,128)}, u32[]{:S(2)}) copy-start(f32[64,4096]{1,0:T(8,128)} %all-reduce.3.cloned.1.call-done) | copy-start | bytes 3145732
  451.2 248.0 %copy-start.6 = (f32[4096]{0:T(1024)S(1)}, f32[4096]{0:T(1024)}, u32[]{:S(2)}) copy-start(f32[4096]{0:T(1024)} %copy-done.5) | copy-start | bytes 49156
  568.4 1.0 copy-start.3
  759.8 1.0 copy-start.4
Sparse Core Ops, SparseCore 0:
  319.6 130.2 all-reduce.2
  569.6 129.6 all-reduce.4
